TPU v7x, 128 devices: a whole 4x4x4 slice. The times are simulated.
128 devices in a mesh: grp: 8 (over z, y_lo), dev: 16 (over x, y_hi, core).
Axes of the slice: x: 4, y: 4 (y_hi: 2, y_lo: 2; y = y_hi * 2 + y_lo), z: 4, core: 2. Of those that a mesh axis runs over, the one named last changes fastest.
Arguments:
- vertex_values: bfloat16 [8192, 128, 256], P(('grp', 'dev')), may hold values from -6 to 6
- position_domain_label: int32 [8192], P(('grp', 'dev')), may hold values from 0 to 64, as said below
- position_vertex_tally: int32 [8192], P(('grp', 'dev')), may hold values from 0 to 128, as said below
- normalizer_gain: float32 [256], replicated, may hold values from 0.1 to 1.9
- embedding_matrix: bfloat16 [256, 256], replicated, may hold values from -0.375 to 0.375
- partition_input_matrix: bfloat16 [256, 256], replicated, may hold values from -0.375 to 0.375
- partition_score_matrix: bfloat16 [32, 64], replicated, may hold values from -60 to 60
- softmax_sharpness: float32 [8], replicated, may hold values from 0.3 to 1
- partition_attention_maps: float32 [3, 32, 32], replicated, may hold values from -10 to 10
- readout_matrix: bfloat16 [256, 256], replicated, may hold values from -1.5 to 1.5
Outputs:
- updated: bfloat16 [8192, 128, 256], P(('grp', 'dev'))
Inputs may be any that keep to these rules, and one draw needn't show every extreme that they name: `position_domain_label`: on each device the used slots come first; a device may use none. Reading the devices in order and their used slots in order lists every mesh's blocks as one run, meshes in increasing order, each mesh 2 or more blocks. Exactly 4096 slots are used in all, and some device uses all 64 of its slots. `position_vertex_tally`: 128 in every used slot except the last block of each mesh, which holds 1 to 128; 0 in unused slots.
All inputs are finite; a program needn't handle non-finite values.
Results may differ from a plain program's by a relative error of at most 0.012.
The roundings to bfloat16 on the way count: a program that leaves them out, or rounds other values in their place, can miss the bound.
Values may be sent and summed in bfloat16 or wider, within the bound.
No kernel may reach another device: no remote copies, remote signals or barrier semaphores. Data moves between devices by JAX's collectives and lax.ppermute only.
A program may use at most 128 MiB of HBM per device.

v0:
```python
import jax
import jax.numpy as jnp
from jax import lax
from jax.sharding import PartitionSpec as P

MESHES = 64


def partition_routine(
    tile_sequence,
    vertex_tallies,
    domain_sequence,
    normalizer_gain,
    embedding_matrix,
    partition_input_matrix,
    partition_score_matrix,
    softmax_sharpness,
):
    tile_amount, tile_height, model_width = tile_sequence.shape
    attention_group_amount = softmax_sharpness.shape[0]
    head_width = model_width // attention_group_amount
    partition_amount = partition_score_matrix.shape[1]
    flattened = tile_sequence.reshape(tile_amount * tile_height, model_width).astype(jnp.float32)
    centre = flattened - jnp.mean(flattened, axis=1, keepdims=True)
    spread = jnp.mean(centre * centre, axis=1, keepdims=True)
    normed = (centre * lax.rsqrt(spread + 1e-05) * normalizer_gain).astype(jnp.bfloat16)
    features = jnp.dot(normed, embedding_matrix, preferred_element_type=jnp.float32).astype(
        jnp.bfloat16
    )
    middles = jnp.dot(normed, partition_input_matrix, preferred_element_type=jnp.float32).astype(
        jnp.bfloat16
    )
    partition_scores = jnp.dot(
        middles.reshape(-1, head_width), partition_score_matrix, preferred_element_type=jnp.float32
    )
    partition_scores = (
        partition_scores.reshape(tile_amount, tile_height, attention_group_amount, partition_amount)
        / softmax_sharpness[:, None]
    )
    living = (
        lax.broadcasted_iota(jnp.int32, (tile_amount, tile_height), 1) < vertex_tallies[:, None]
    ).astype(jnp.float32)
    partition_shares = (
        jax.nn.softmax(partition_scores, axis=-1) * living[:, :, None, None]
    ).astype(jnp.bfloat16)
    partial_sums = jnp.einsum(
        "bphm,bphd->bhmd",
        partition_shares,
        features.reshape(tile_amount, tile_height, attention_group_amount, head_width),
        preferred_element_type=jnp.float32,
    )
    partial_totals = jnp.sum(partition_shares.astype(jnp.float32), axis=1)
    one_hot = (
        domain_sequence[:, None] == lax.broadcasted_iota(jnp.int32, (tile_amount, MESHES), 1)
    ).astype(jnp.float32)
    domain_accumulated = jnp.dot(one_hot.T, partial_sums.reshape(tile_amount, -1))
    domain_share_accumulated = jnp.dot(one_hot.T, partial_totals.reshape(tile_amount, -1))
    return (
        partition_shares.reshape(
            tile_amount, tile_height, attention_group_amount * partition_amount
        ),
        domain_accumulated,
        domain_share_accumulated,
    )


def attend_tokens(domain_accumulated, domain_share_accumulated, partition_attention_maps):
    row_count, partition_amount = domain_share_accumulated.shape
    head_width = partition_attention_maps.shape[1]
    tokens = domain_accumulated.reshape(row_count, partition_amount, head_width) / (
        domain_share_accumulated[:, :, None] + 1.0
    )
    queries = jnp.einsum("rmd,de->rme", tokens, partition_attention_maps[0])
    key_rows = jnp.einsum("rmd,de->rme", tokens, partition_attention_maps[1])
    values = jnp.einsum("rmd,de->rme", tokens, partition_attention_maps[2])
    scores = jnp.einsum("rme,rne->rmn", queries, key_rows) * head_width ** (-0.5)
    token_probs = jax.nn.softmax(scores, axis=-1)
    blended = jnp.einsum("rmn,rne->rme", token_probs, values)
    return blended.reshape(row_count, partition_amount * head_width).astype(jnp.bfloat16)


def spread_phase(
    tile_sequence, vertex_tallies, domain_sequence, partition_shares, tokens, readout_matrix
):
    tile_amount, tile_height, model_width = tile_sequence.shape
    attention_group_amount = tokens.shape[0] // MESHES
    partition_amount = partition_shares.shape[2] // attention_group_amount
    head_width = model_width // attention_group_amount
    tables = tokens.reshape(MESHES, attention_group_amount, partition_amount, head_width)
    chosen = jnp.take(tables, jnp.minimum(domain_sequence, MESHES - 1), axis=0)
    blended = jnp.einsum(
        "bphm,bhmd->bphd",
        partition_shares.reshape(
            tile_amount, tile_height, attention_group_amount, partition_amount
        ),
        chosen,
        preferred_element_type=jnp.float32,
    ).astype(jnp.bfloat16)
    projected = jnp.dot(
        blended.reshape(-1, model_width), readout_matrix, preferred_element_type=jnp.float32
    )
    living = (
        lax.broadcasted_iota(jnp.int32, (tile_amount, tile_height), 1) < vertex_tallies[:, None]
    ).astype(jnp.float32)
    result = (
        tile_sequence.reshape(-1, model_width).astype(jnp.float32) + projected
    ) * living.reshape(-1, 1)
    return result.reshape(tile_amount, tile_height, model_width).astype(jnp.bfloat16)


def on_device(
    vertex_values,
    position_domain_label,
    position_vertex_tally,
    normalizer_gain,
    embedding_matrix,
    partition_input_matrix,
    partition_score_matrix,
    softmax_sharpness,
    partition_attention_maps,
    readout_matrix,
):
    slot_total, tile_height, model_width = vertex_values.shape
    attention_group_amount = softmax_sharpness.shape[0]
    partition_amount = partition_score_matrix.shape[1]
    group_count = slot_total // 16
    grouped = (
        vertex_values.reshape(group_count, 16, tile_height, model_width),
        position_vertex_tally.reshape(group_count, 16),
        position_domain_label.reshape(group_count, 16),
    )

    def gather_step(running, lookup_element):
        partition_shares, domain_accumulated, domain_share_accumulated = partition_routine(
            lookup_element[0],
            lookup_element[1],
            lookup_element[2],
            normalizer_gain,
            embedding_matrix,
            partition_input_matrix,
            partition_score_matrix,
            softmax_sharpness,
        )
        return (
            (running[0] + domain_accumulated, running[1] + domain_share_accumulated),
            partition_shares,
        )

    initial = (
        jnp.zeros((MESHES, model_width * partition_amount), jnp.float32),
        jnp.zeros((MESHES, attention_group_amount * partition_amount), jnp.float32),
    )
    (domain_accumulated, domain_share_accumulated), partition_shares = lax.scan(
        gather_step, initial, grouped
    )
    whole_sums, whole_totals = lax.psum(
        (
            domain_accumulated.reshape(MESHES * attention_group_amount, -1),
            domain_share_accumulated.reshape(MESHES * attention_group_amount, -1),
        ),
        ("grp", "dev"),
    )
    tokens = attend_tokens(whole_sums, whole_totals, partition_attention_maps)

    def spread_step(lookup_element):
        return spread_phase(
            lookup_element[0],
            lookup_element[1],
            lookup_element[2],
            lookup_element[3],
            tokens,
            readout_matrix,
        )

    return lax.map(spread_step, grouped + (partition_shares,)).reshape(vertex_values.shape)


def solution(mesh):
    return jax.shard_map(
        on_device,
        mesh=mesh,
        in_specs=(
            P(("grp", "dev"), None, None),
            P(("grp", "dev")),
            P(("grp", "dev")),
            P(),
            P(),
            P(),
            P(),
            P(),
            P(),
            P(),
        ),
        out_specs=P(("grp", "dev"), None, None),
        check_vma=False,
    )
```

profile of v0, /device:TPU:1, one launch (start us, length us, event | category | flops | bytes accessed | tf_op | source)
XLA Modules:
  0.0 490.3 jit_solution(10821527517631763876)
XLA Ops:
  8.0 115.3 %while.26 = (s32[]{:T(128)}, f32[64,16384]{1,0:T(8,128)}, f32[64,512]{1,0:T(8,128)S(1)}, bf16[4,16,128,512]{2,3,1,0:T(8,128)(2,1)}, s32[4,16]{1,0:T(4,128)S(1)},...) while((s32[]{:T(128)}, f32[64,16384]{1,0:T(8,128)}, ...), condition=%wide.region_6.7_spmd.clone, body=%wide.region_0.6_spmd.clone.sunk | while | flops 723058752 | bytes 48028012 | solution.py:153
  9.6 1.9 multiply_reduce_fusion.3
  11.6 1.8 fusion.110
  14.7 3.6 fusion.111
  18.4 3.4 convert_reduce_fusion.5
  24.9 2.1 fusion.112
  27.0 3.5 reshape.222
  30.5 2.8 convolution_add_fusion.5
  35.2 1.6 convert_reduce_fusion.4
  36.9 1.9 multiply_reduce_fusion.3
  38.8 1.8 fusion.110
  41.9 3.6 fusion.111
  45.6 3.4 convert_reduce_fusion.5
  52.1 2.1 fusion.112
  54.2 3.5 reshape.222
  57.7 5.0 %convolution_add_fusion.5 = f32[64,16384]{1,0:T(8,128)} fusion(bf16[16,16384]{1,0:T(8,128)(2,1)S(1)} %reshape.222, f32[64,16384]{1,0:T(8,128)} %get-tuple-element.383, pred[]{:T(512)S(6)} %compare.3, s32[16]{0:T(128)S(1)} %get-tuple-element.366), kind=kOutput, calls=%fused_computation.27.clone.1 | convolution fusion | flops 35652608 | bytes 8912961 | tf_op jit(solution)/shard_map/while/body/eval_jaxpr/dot_general | solution.py:56
  66.2 1.9 multiply_reduce_fusion.3
  68.1 1.8 fusion.110
  71.3 3.6 fusion.111
  74.9 3.4 convert_reduce_fusion.5
  81.5 2.1 fusion.112
  83.5 3.5 reshape.222
  87.0 5.0 %convolution_add_fusion.5 = f32[64,16384]{1,0:T(8,128)} fusion(bf16[16,16384]{1,0:T(8,128)(2,1)S(1)} %reshape.222, f32[64,16384]{1,0:T(8,128)} %get-tuple-element.383, pred[]{:T(512)S(6)} %compare.3, s32[16]{0:T(128)S(1)} %get-tuple-element.366), kind=kOutput, calls=%fused_computation.27.clone.1 | convolution fusion | flops 35652608 | bytes 8912961 | tf_op jit(solution)/shard_map/while/body/eval_jaxpr/dot_general | solution.py:56
  95.6 1.9 multiply_reduce_fusion.3
  97.5 1.8 fusion.110
  100.6 3.6 fusion.111
  104.3 3.4 convert_reduce_fusion.5
  110.8 2.1 fusion.112
  112.9 3.5 reshape.222
  116.4 5.0 %convolution_add_fusion.5 = f32[64,16384]{1,0:T(8,128)} fusion(bf16[16,16384]{1,0:T(8,128)(2,1)S(1)} %reshape.222, f32[64,16384]{1,0:T(8,128)} %get-tuple-element.383, pred[]{:T(512)S(6)} %compare.3, s32[16]{0:T(128)S(1)} %get-tuple-element.366), kind=kOutput, calls=%fused_computation.27.clone.1 | convolution fusion | flops 35652608 | bytes 8912961 | tf_op jit(solution)/shard_map/while/body/eval_jaxpr/dot_general | solution.py:56
  123.3 5.0 %reshape.192 = f32[512,2048]{1,0:T(8,128)} reshape(f32[64,16384]{1,0:T(8,128)} %get-tuple-element.111) | data formatting | bytes 8388608 | tf_op jit(solution)/shard_map/reshape | solution.py:158
  129.2 157.6 %all-reduce.3.cloned.1.call-done = (f32[512,2048]{1,0:T(8,128)}, f32[512,64]{0,1:T(8,128)}) async-done(((f32[512,2048]{1,0:T(8,128)}, f32[512,64]{0,1:T(8,128)}), (f32[512,2048]{1,0:T(8,128)}, f32[512,64]{0,1:T(8,128)})) %all-reduce.3.cloned.1.call-update) | async-done | bytes 4325392 | tf_op jit(solution)/shard_map/psum | solution.py:156
  287.8 2.5 div.47
  290.3 5.4 %copy.52 = f32[512,2048]{1,0:T(8,128)} copy(f32[512,2048]{0,1:T(8,128)} %bitcast.167) | data formatting | bytes 8388608 | tf_op jit(solution)/shard_map/div | solution.py:70
  295.7 5.7 %div.49 = bf16[512,2048]{1,0:T(8,128)(2,1)} divide(f32[512,2048]{1,0:T(8,128)} %get-tuple-element.218, f32[512,2048]{1,0:T(8,128)} %copy.52) | non-fusion elementwise | flops 1048576 | bytes 10485760 | tf_op jit(solution)/shard_map/div | solution.py:70
  301.3 3.0 copy.53
  304.4 2.1 fusion.39
  306.5 2.0 fusion.37
  308.5 2.1 fusion.35
  310.6 8.8 %copy.56 = bf16[512,64,32]{1,2,0:T(8,128)(2,1)} copy(bf16[512,64,32]{0,2,1:T(8,128)(2,1)} %fusion.39) | data formatting | bytes 4194304 | tf_op jit(solution)/shard_map/rmd,de->rme/dot_general | solution.py:73
  319.3 8.9 %copy.57 = bf16[512,64,32]{1,2,0:T(8,128)(2,1)} copy(bf16[512,64,32]{0,2,1:T(8,128)(2,1)} %fusion.37) | data formatting | bytes 4194304 | tf_op jit(solution)/shard_map/rmd,de->rme/dot_general | solution.py:74
  328.3 7.9 %copy.60 = bf16[512,64,32]{1,2,0:T(8,128)(2,1)} copy(bf16[512,64,32]{0,2,1:T(8,128)(2,1)S(1)} %copy-done) | data formatting | bytes 4194304 | tf_op jit(solution)/shard_map/rmd,de->rme/dot_general | solution.py:75
  336.1 12.5 %multiply_reduce_fusion.1 = (f32[512,64]{1,0:T(8,128)S(1)}, f32[512,64,64]{1,2,0:T(8,128)}) fusion(bf16[512,64,32]{1,2,0:T(8,128)(2,1)} %copy.56, bf16[512,64,32]{1,2,0:T(8,128)(2,1)} %copy.57), kind=kOutput, calls=%fused_computation.61 | convolution fusion | flops 138379264 | bytes 12713984 | tf_op jit(solution)/shard_map/rme,rne->rmn/dot_general | solution.py:76
  348.7 10.3 %fusion.28 = f32[512,64]{1,0:T(8,128)S(1)} fusion(f32[512,64,64]{1,2,0:T(8,128)} %get-tuple-element.229, f32[512,64]{1,0:T(8,128)S(1)} %get-tuple-element.228), kind=kLoop, calls=%fused_computation.62 | loop fusion | flops 6258688 | bytes 8650752 | tf_op jit(solution)/shard_map/reduce_sum | solution.py:77
  359.0 10.4 %fusion.32 = bf16[512,64,32]{1,2,0:T(8,128)(2,1)} fusion(bf16[512,64,32]{1,2,0:T(8,128)(2,1)} %copy.60, f32[512,64,64]{1,2,0:T(8,128)} %get-tuple-element.229, f32[512,64]{1,0:T(8,128)S(1)} %fusion.28, f32[512,64]{1,0:T(8,128)S(1)} %get-tuple-element.228), kind=kOutput, calls=%fused_computation.66 | convolution fusion | flops 140509184 | bytes 12845056 | tf_op jit(solution)/shard_map/rmn,rne->rme/dot_general | solution.py:78
  369.4 6.9 %copy.61 = bf16[512,64,32]{0,2,1:T(8,128)(2,1)} copy(bf16[512,64,32]{1,2,0:T(8,128)(2,1)} %fusion.32) | data formatting | bytes 4194304 | tf_op jit(solution)/shard_map/convert_element_type | solution.py:79
  376.3 2.9 copy.62
  379.3 104.2 %while.25 = (s32[]{:T(128)}, bf16[4,16,128,256]{3,2,1,0:T(8,128)(2,1)}, bf16[4,16,128,256]{3,2,1,0:T(8,128)(2,1)}, s32[4,16]{1,0:T(4,128)S(1)}, bf16[512,2048]{1...) while((s32[]{:T(128)}, ...), condition=%wide.region_12.13_spmd, body=%wide.region_11.12_spmd.sunk | while | flops 338433216 | bytes 26891408 | solution.py:175
  379.6 8.0 %reshape.221 = bf16[64,8,64,32]{3,2,1,0:T(8,128)(2,1)} reshape(bf16[512,2048]{1,0:T(8,128)(2,1)S(1)} %get-tuple-element.432) | data formatting | bytes 4194304 | tf_op jit(solution)/shard_map/while/body/eval_jaxpr/reshape | solution.py:89
  387.6 8.6 %copy.92 = bf16[64,8,64,32]{2,3,1,0:T(8,128)(2,1)} copy(bf16[64,8,64,32]{3,2,1,0:T(8,128)(2,1)} %reshape.221) | data formatting | bytes 4194304 | tf_op jit(solution)/shard_map/while/body/eval_jaxpr/reshape | solution.py:89
  396.2 2.9 gather_fusion
  399.1 1.8 constant_dynamic-slice_fusion.9
  405.6 8.0 %reshape.221 = bf16[64,8,64,32]{3,2,1,0:T(8,128)(2,1)} reshape(bf16[512,2048]{1,0:T(8,128)(2,1)S(1)} %get-tuple-element.432) | data formatting | bytes 4194304 | tf_op jit(solution)/shard_map/while/body/eval_jaxpr/reshape | solution.py:89
  413.6 8.6 %copy.92 = bf16[64,8,64,32]{2,3,1,0:T(8,128)(2,1)} copy(bf16[64,8,64,32]{3,2,1,0:T(8,128)(2,1)} %reshape.221) | data formatting | bytes 4194304 | tf_op jit(solution)/shard_map/while/body/eval_jaxpr/reshape | solution.py:89
  422.2 2.9 gather_fusion
  425.1 1.8 constant_dynamic-slice_fusion.9
  431.5 8.0 %reshape.221 = bf16[64,8,64,32]{3,2,1,0:T(8,128)(2,1)} reshape(bf16[512,2048]{1,0:T(8,128)(2,1)S(1)} %get-tuple-element.432) | data formatting | bytes 4194304 | tf_op jit(solution)/shard_map/while/body/eval_jaxpr/reshape | solution.py:89
  439.6 8.6 %copy.92 = bf16[64,8,64,32]{2,3,1,0:T(8,128)(2,1)} copy(bf16[64,8,64,32]{3,2,1,0:T(8,128)(2,1)} %reshape.221) | data formatting | bytes 4194304 | tf_op jit(solution)/shard_map/while/body/eval_jaxpr/reshape | solution.py:89
  448.2 2.9 gather_fusion
  451.1 1.8 constant_dynamic-slice_fusion.9
  457.5 8.0 %reshape.221 = bf16[64,8,64,32]{3,2,1,0:T(8,128)(2,1)} reshape(bf16[512,2048]{1,0:T(8,128)(2,1)S(1)} %get-tuple-element.432) | data formatting | bytes 4194304 | tf_op jit(solution)/shard_map/while/body/eval_jaxpr/reshape | solution.py:89
  465.6 8.6 %copy.92 = bf16[64,8,64,32]{2,3,1,0:T(8,128)(2,1)} copy(bf16[64,8,64,32]{3,2,1,0:T(8,128)(2,1)} %reshape.221) | data formatting | bytes 4194304 | tf_op jit(solution)/shard_map/while/body/eval_jaxpr/reshape | solution.py:89
  474.1 2.9 gather_fusion
  477.1 1.8 constant_dynamic-slice_fusion.9
  (144 shorter events, 52.2 us)
Async XLA Ops:
  6.5 280.3 %all-reduce.3.cloned.1.call-start = ((), (), s32[]{:S(2)}) async-start(), calls=%async_computation | async-start | bytes 8650752 | tf_op jit(solution)/shard_map/psum | solution.py:156
  8.0 5.3 %copy-start.1 = (bf16[256,256]{1,0:T(8,128)(2,1)S(1)}, bf16[256,256]{1,0:T(8,128)(2,1)}, u32[]{:S(2)}) copy-start(bf16[256,256]{1,0:T(8,128)(2,1)} %get-tuple-element.403) | copy-start | bytes 393220 | tf_op jit(solution)/shard_map/while
  11.5 3.1 copy-start.5
  11.5 3.1 copy-start.6
  18.3 3.5 copy-start.2
  35.2 5.3 %copy-start.1 = (bf16[256,256]{1,0:T(8,128)(2,1)S(1)}, bf16[256,256]{1,0:T(8,128)(2,1)}, u32[]{:S(2)}) copy-start(bf16[256,256]{1,0:T(8,128)(2,1)} %get-tuple-element.403) | copy-start | bytes 393220 | tf_op jit(solution)/shard_map/while
  38.8 3.1 copy-start.5
  38.8 3.1 copy-start.6
  45.5 3.5 copy-start.2
  64.6 5.3 %copy-start.1 = (bf16[256,256]{1,0:T(8,128)(2,1)S(1)}, bf16[256,256]{1,0:T(8,128)(2,1)}, u32[]{:S(2)}) copy-start(bf16[256,256]{1,0:T(8,128)(2,1)} %get-tuple-element.403) | copy-start | bytes 393220 | tf_op jit(solution)/shard_map/while
  68.1 3.1 copy-start.5
  68.1 3.1 copy-start.6
  74.8 3.5 copy-start.2
  94.0 5.3 %copy-start.1 = (bf16[256,256]{1,0:T(8,128)(2,1)S(1)}, bf16[256,256]{1,0:T(8,128)(2,1)}, u32[]{:S(2)}) copy-start(bf16[256,256]{1,0:T(8,128)(2,1)} %get-tuple-element.403) | copy-start | bytes 393220 | tf_op jit(solution)/shard_map/while
  97.5 3.1 copy-start.5
  97.5 3.1 copy-start.6
  104.2 3.5 copy-start.2
  301.3 3.1 copy-start.3
  319.3 8.9 %copy-start = (bf16[512,64,32]{0,2,1:T(8,128)(2,1)S(1)}, bf16[512,64,32]{0,2,1:T(8,128)(2,1)}, u32[]{:S(2)}) copy-start(bf16[512,64,32]{0,2,1:T(8,128)(2,1)} %fusion.35) | copy-start | bytes 6291460
  369.4 9.9 %copy-start.4 = (bf16[256,256]{1,0:T(8,128)(2,1)S(1)}, bf16[256,256]{1,0:T(8,128)(2,1)}, u32[]{:S(2)}) copy-start(bf16[256,256]{1,0:T(8,128)(2,1)} %param.23) | copy-start | bytes 393220
Sparse Core Ops, SparseCore 0:
  129.3 157.4 all-reduce.2
where the time goes:
time: 493 us; the launch traced here: 490 us
  local copies, waits for them, and re-layouts  182 us (37%)
  waiting for transfers between devices  158 us (32%)
  matrix products  84 us (17%)
  other arithmetic  52.1 us (11%)
  between operations  13.5 us (3%)
    psum x1, waiting for transfers between devices, on_device(): lax.psum((domain_accumulated.reshape(MESHES * attention_group_amount, -1)...  158 us
    reshape x8, local copies, waits for them, and re-layouts, spread_phase(): tokens.reshape(MESHES, attention_group_amount, partition_amount, head_width)  66.4 us
    dot_general x4, matrix products, partition_routine(): jnp.dot(one_hot.T, partial_sums.reshape(tile_amount, -1))  17.9 us
    sub x4, matrix products, partition_routine(): jax.nn.softmax(partition_scores, axis=-1) * living[:, :, None, None]  14.4 us
    reshape x4, local copies, waits for them, and re-layouts, partition_routine(): partial_sums.reshape(tile_amount, -1)  14 us
    reduce_sum x4, other arithmetic, partition_routine(): partial_totals = jnp.sum(partition_shares.astype(jnp.float32), axis=1)  13.5 us
    dot_general x1, matrix products, attend_tokens(): jnp.einsum('rme,rne->rmn', queries, key_rows) * head_width ** (-0.5)  12.5 us
    gather x4, local copies, waits for them, and re-layouts, spread_phase(): chosen = jnp.take(tables, jnp.minimum(domain_sequence, MESHES - 1), axis=0)  11.7 us
  transfers between devices with their start and end apart: 1, of which 1 were waited for; matrix products, arithmetic and copies ran while one was open for 0% of the time, Pallas kernels for 0%

commit v1 on v0

--- a/solution.py
+++ b/solution.py
@@ -4,6 +4,11 @@
 from jax.sharding import PartitionSpec as P
 
 MESHES = 64
+
+
+def one_after_other(value, one, other):
+    inner = lax.psum(value, one)
+    return lax.psum(inner, other)
 
 
 def partition_routine(
@@ -153,12 +158,13 @@
     (domain_accumulated, domain_share_accumulated), partition_shares = lax.scan(
         gather_step, initial, grouped
     )
-    whole_sums, whole_totals = lax.psum(
+    whole_sums, whole_totals = one_after_other(
         (
             domain_accumulated.reshape(MESHES * attention_group_amount, -1),
             domain_share_accumulated.reshape(MESHES * attention_group_amount, -1),
         ),
-        ("grp", "dev"),
+        "dev",
+        "grp",
     )
     tokens = attend_tokens(whole_sums, whole_totals, partition_attention_maps)
 

time: 493 us -> 682 us (1.38)
  waiting for transfers between devices: 158 us -> 347 us
    psum x1 -> x2, waiting for transfers between devices: 158 us -> 347 us  [the longest x1 192 us: one_after_other(): return lax.psum(inner, other)]
  transfers between devices with their start and end apart: 1 -> 2, of which waited for: 1 -> 2; matrix products, arithmetic and copies ran while one was open for 0% -> 0% of each run, Pallas kernels for 0% -> 0%
where the time goes in v1:
time: 682 us; the launch traced here: 679 us
  waiting for transfers between devices  347 us (51%)
  local copies, waits for them, and re-layouts  182 us (27%)
  matrix products  84 us (12%)
  other arithmetic  52.1 us (8%)
  between operations  13.5 us (2%)
    psum x1, waiting for transfers between devices, one_after_other(): return lax.psum(inner, other)  192 us
    psum x1, waiting for transfers between devices, one_after_other(): inner = lax.psum(value, one)  155 us
    reshape x8, local copies, waits for them, and re-layouts, spread_phase(): tokens.reshape(MESHES, attention_group_amount, partition_amount, head_width)  66.4 us
    dot_general x4, matrix products, partition_routine(): jnp.dot(one_hot.T, partial_sums.reshape(tile_amount, -1))  17.9 us
    sub x4, matrix products, partition_routine(): jax.nn.softmax(partition_scores, axis=-1) * living[:, :, None, None]  14.4 us
    reshape x4, local copies, waits for them, and re-layouts, partition_routine(): partial_sums.reshape(tile_amount, -1)  14 us
  transfers between devices with their start and end apart: 2, of which 2 were waited for; matrix products, arithmetic and copies ran while one was open for 0% of the time, Pallas kernels for 0%

profile of v1, /device:TPU:1, one launch (start us, length us, event | category | flops | bytes accessed | tf_op | source)
XLA Modules:
  0.0 679.4 jit_solution(11537528377936239577)
XLA Ops:
  8.0 115.3 %while.26 = (s32[]{:T(128)}, f32[64,16384]{1,0:T(8,128)}, f32[64,512]{1,0:T(8,128)S(1)}, bf16[4,16,128,512]{2,3,1,0:T(8,128)(2,1)}, s32[4,16]{1,0:T(4,128)S(1)},...) while((s32[]{:T(128)}, f32[64,16384]{1,0:T(8,128)}, ...), condition=%wide.region_6.7_spmd.clone, body=%wide.region_0.6_spmd.clone.sunk | while | flops 723058752 | bytes 48028012 | solution.py:158
  9.6 1.9 multiply_reduce_fusion.3
  11.6 1.8 fusion.110
  14.7 3.6 fusion.111
  18.4 3.4 convert_reduce_fusion.5
  24.9 2.1 fusion.112
  27.0 3.5 reshape.222
  30.5 2.8 convolution_add_fusion.5
  36.9 1.9 multiply_reduce_fusion.3
  38.8 1.8 fusion.110
  41.9 3.6 fusion.111
  45.6 3.4 convert_reduce_fusion.5
  52.1 2.1 fusion.112
  54.2 3.5 reshape.222
  57.7 5.0 convolution_add_fusion.5
  66.2 1.9 multiply_reduce_fusion.3
  68.1 1.8 fusion.110
  71.3 3.6 fusion.111
  74.9 3.4 convert_reduce_fusion.5
  81.5 2.1 fusion.112
  83.5 3.5 reshape.222
  87.0 5.0 convolution_add_fusion.5
  95.6 1.9 multiply_reduce_fusion.3
  97.5 1.8 fusion.110
  100.6 3.6 fusion.111
  104.3 3.4 convert_reduce_fusion.5
  110.8 2.1 fusion.112
  112.9 3.5 reshape.222
  116.4 5.0 convolution_add_fusion.5
  123.3 4.9 reshape.192
  129.4 154.9 %all-reduce.5.cloned.1.call-done = (f32[512,2048]{1,0:T(8,128)}, f32[512,64]{0,1:T(8,128)}) async-done(((f32[512,2048]{1,0:T(8,128)}, f32[512,64]{0,1:T(8,128)}), (f32[512,2048]{1,0:T(8,128)}, f32[512,64]{0,1:T(8,128)})) %all-reduce.5.cloned.1.call-update) | async-done | bytes 4325392 | tf_op jit(solution)/shard_map/psum | solution.py:10
  284.3 191.7 %all-reduce.7.cloned.1.call-done = (f32[512,2048]{1,0:T(8,128)}, f32[512,64]{0,1:T(8,128)}) async-done(((f32[512,2048]{1,0:T(8,128)}, f32[512,64]{0,1:T(8,128)}), (f32[512,2048]{1,0:T(8,128)}, f32[512,64]{0,1:T(8,128)})) %all-reduce.7.cloned.1.call-update) | async-done | bytes 4325392 | tf_op jit(solution)/shard_map/psum | solution.py:11
  477.0 2.5 div.47
  479.5 5.4 copy.52
  484.9 5.7 div.49
  490.5 2.9 copy.53
  493.4 2.1 fusion.39
  495.5 2.0 fusion.37
  497.5 2.1 fusion.35
  499.6 8.8 %copy.56 = bf16[512,64,32]{1,2,0:T(8,128)(2,1)} copy(bf16[512,64,32]{0,2,1:T(8,128)(2,1)} %fusion.39) | data formatting | bytes 4194304 | tf_op jit(solution)/shard_map/rmd,de->rme/dot_general | solution.py:78
  508.4 8.9 %copy.57 = bf16[512,64,32]{1,2,0:T(8,128)(2,1)} copy(bf16[512,64,32]{0,2,1:T(8,128)(2,1)} %fusion.37) | data formatting | bytes 4194304 | tf_op jit(solution)/shard_map/rmd,de->rme/dot_general | solution.py:79
  517.3 7.9 %copy.60 = bf16[512,64,32]{1,2,0:T(8,128)(2,1)} copy(bf16[512,64,32]{0,2,1:T(8,128)(2,1)S(1)} %copy-done) | data formatting | bytes 4194304 | tf_op jit(solution)/shard_map/rmd,de->rme/dot_general | solution.py:80
  525.2 12.5 %multiply_reduce_fusion.1 = (f32[512,64]{1,0:T(8,128)S(1)}, f32[512,64,64]{1,2,0:T(8,128)}) fusion(bf16[512,64,32]{1,2,0:T(8,128)(2,1)} %copy.56, bf16[512,64,32]{1,2,0:T(8,128)(2,1)} %copy.57), kind=kOutput, calls=%fused_computation.61 | convolution fusion | flops 138379264 | bytes 12713984 | tf_op jit(solution)/shard_map/rme,rne->rmn/dot_general | solution.py:81
  537.7 10.3 %fusion.28 = f32[512,64]{1,0:T(8,128)S(1)} fusion(f32[512,64,64]{1,2,0:T(8,128)} %get-tuple-element.231, f32[512,64]{1,0:T(8,128)S(1)} %get-tuple-element.230), kind=kLoop, calls=%fused_computation.62 | loop fusion | flops 6258688 | bytes 8650752 | tf_op jit(solution)/shard_map/reduce_sum | solution.py:82
  548.0 10.4 %fusion.32 = bf16[512,64,32]{1,2,0:T(8,128)(2,1)} fusion(bf16[512,64,32]{1,2,0:T(8,128)(2,1)} %copy.60, f32[512,64,64]{1,2,0:T(8,128)} %get-tuple-element.231, f32[512,64]{1,0:T(8,128)S(1)} %fusion.28, f32[512,64]{1,0:T(8,128)S(1)} %get-tuple-element.230), kind=kOutput, calls=%fused_computation.66 | convolution fusion | flops 140509184 | bytes 12845056 | tf_op jit(solution)/shard_map/rmn,rne->rme/dot_general | solution.py:83
  558.4 6.9 %copy.61 = bf16[512,64,32]{0,2,1:T(8,128)(2,1)} copy(bf16[512,64,32]{1,2,0:T(8,128)(2,1)} %fusion.32) | data formatting | bytes 4194304 | tf_op jit(solution)/shard_map/convert_element_type | solution.py:84
  565.4 2.9 copy.62
  568.3 104.2 %while.25 = (s32[]{:T(128)}, bf16[4,16,128,256]{3,2,1,0:T(8,128)(2,1)}, bf16[4,16,128,256]{3,2,1,0:T(8,128)(2,1)}, s32[4,16]{1,0:T(4,128)S(1)}, bf16[512,2048]{1...) while((s32[]{:T(128)}, ...), condition=%wide.region_14.15_spmd, body=%wide.region_13.14_spmd.sunk | while | flops 338433216 | bytes 26891408 | solution.py:181
  568.6 8.0 %reshape.221 = bf16[64,8,64,32]{3,2,1,0:T(8,128)(2,1)} reshape(bf16[512,2048]{1,0:T(8,128)(2,1)S(1)} %get-tuple-element.434) | data formatting | bytes 4194304 | tf_op jit(solution)/shard_map/while/body/eval_jaxpr/reshape | solution.py:94
  576.7 8.6 %copy.92 = bf16[64,8,64,32]{2,3,1,0:T(8,128)(2,1)} copy(bf16[64,8,64,32]{3,2,1,0:T(8,128)(2,1)} %reshape.221) | data formatting | bytes 4194304 | tf_op jit(solution)/shard_map/while/body/eval_jaxpr/reshape | solution.py:94
  585.2 2.9 gather_fusion
  588.2 1.8 constant_dynamic-slice_fusion.9
  594.6 8.0 %reshape.221 = bf16[64,8,64,32]{3,2,1,0:T(8,128)(2,1)} reshape(bf16[512,2048]{1,0:T(8,128)(2,1)S(1)} %get-tuple-element.434) | data formatting | bytes 4194304 | tf_op jit(solution)/shard_map/while/body/eval_jaxpr/reshape | solution.py:94
  602.6 8.6 %copy.92 = bf16[64,8,64,32]{2,3,1,0:T(8,128)(2,1)} copy(bf16[64,8,64,32]{3,2,1,0:T(8,128)(2,1)} %reshape.221) | data formatting | bytes 4194304 | tf_op jit(solution)/shard_map/while/body/eval_jaxpr/reshape | solution.py:94
  611.2 2.9 gather_fusion
  614.2 1.8 constant_dynamic-slice_fusion.9
  620.6 8.0 %reshape.221 = bf16[64,8,64,32]{3,2,1,0:T(8,128)(2,1)} reshape(bf16[512,2048]{1,0:T(8,128)(2,1)S(1)} %get-tuple-element.434) | data formatting | bytes 4194304 | tf_op jit(solution)/shard_map/while/body/eval_jaxpr/reshape | solution.py:94
  628.6 8.6 %copy.92 = bf16[64,8,64,32]{2,3,1,0:T(8,128)(2,1)} copy(bf16[64,8,64,32]{3,2,1,0:T(8,128)(2,1)} %reshape.221) | data formatting | bytes 4194304 | tf_op jit(solution)/shard_map/while/body/eval_jaxpr/reshape | solution.py:94
  637.2 2.9 gather_fusion
  640.2 1.8 constant_dynamic-slice_fusion.9
  646.6 8.0 %reshape.221 = bf16[64,8,64,32]{3,2,1,0:T(8,128)(2,1)} reshape(bf16[512,2048]{1,0:T(8,128)(2,1)S(1)} %get-tuple-element.434) | data formatting | bytes 4194304 | tf_op jit(solution)/shard_map/while/body/eval_jaxpr/reshape | solution.py:94
  654.6 8.6 %copy.92 = bf16[64,8,64,32]{2,3,1,0:T(8,128)(2,1)} copy(bf16[64,8,64,32]{3,2,1,0:T(8,128)(2,1)} %reshape.221) | data formatting | bytes 4194304 | tf_op jit(solution)/shard_map/while/body/eval_jaxpr/reshape | solution.py:94
  663.2 2.9 gather_fusion
  666.1 1.8 constant_dynamic-slice_fusion.9
  (147 shorter events, 54.1 us)
Async XLA Ops:
  6.5 277.8 %all-reduce.5.cloned.1.call-start = ((), (), s32[]{:S(2)}) async-start(), calls=%async_computation | async-start | bytes 8650752 | tf_op jit(solution)/shard_map/psum | solution.py:10
  8.0 5.3 copy-start.1
  11.5 3.1 copy-start.5
  11.5 3.1 copy-start.6
  18.3 3.5 copy-start.2
  35.2 5.3 copy-start.1
  38.8 3.1 copy-start.5
  38.8 3.1 copy-start.6
  45.5 3.5 copy-start.2
  64.6 5.3 copy-start.1
  68.1 3.1 copy-start.5
  68.1 3.1 copy-start.6
  74.8 3.5 copy-start.2
  93.9 5.3 copy-start.1
  97.5 3.1 copy-start.5
  97.5 3.1 copy-start.6
  104.2 3.5 copy-start.2
  129.2 346.9 %all-reduce.7.cloned.1.call-start = ((), (), s32[]{:S(2)}) async-start(), calls=%async_computation.1 | async-start | bytes 8650752 | tf_op jit(solution)/shard_map/psum | solution.py:11
  490.5 2.9 copy-start.3
  508.4 8.9 %copy-start = (bf16[512,64,32]{0,2,1:T(8,128)(2,1)S(1)}, bf16[512,64,32]{0,2,1:T(8,128)(2,1)}, u32[]{:S(2)}) copy-start(bf16[512,64,32]{0,2,1:T(8,128)(2,1)} %fusion.35) | copy-start | bytes 6291460
  558.4 9.9 %copy-start.4 = (bf16[256,256]{1,0:T(8,128)(2,1)S(1)}, bf16[256,256]{1,0:T(8,128)(2,1)}, u32[]{:S(2)}) copy-start(bf16[256,256]{1,0:T(8,128)(2,1)} %param.23) | copy-start | bytes 393220
Sparse Core Ops, SparseCore 0:
  129.3 154.9 all-reduce.4
  286.9 189.1 all-reduce.6
